TPU v7x, 256 devices: a whole 4x4x8 slice. The times are simulated.
256 devices in a mesh: rep: 32 (over x_hi, z, core), tp: 8 (over x_lo, y).
Axes of the slice: x: 4 (x_hi: 2, x_lo: 2; x = x_hi * 2 + x_lo), y: 4, z: 8, core: 2. Of those that a mesh axis runs over, the one named last changes fastest.
Arguments:
- tokens: bfloat16 [32, 1024, 3072], P('rep', 'tp'), may hold values from -100 to 100
- norm_gain: float32 [32, 3072], P('rep'), may hold values from 0.5 to 1.5
- w_query: bfloat16 [32, 3072, 2048], P('rep', None, 'tp'), may hold values from -1 to 1
- key_weight: bfloat16 [32, 3072, 1024], P('rep', None, 'tp'), may hold values from -1 to 1
- value_weight: bfloat16 [32, 3072, 1024], P('rep', None, 'tp'), may hold values from -0.109375 to 0.109375
- attention_gradient: bfloat16 [32, 1024, 2048], P('rep', None, 'tp'), may hold values from -6 to 6
- global_fragment: float32 [512, 3072], P('tp'), may hold values from -6 to 6
- momentum: float32 [512, 3072], P('tp'), may hold values from -3 to 3
- local_fragment: bfloat16 [32, 512, 3072], P('rep', 'tp'), may hold values from -6 to 6
Outputs:
- grad_query_w: bfloat16 [32, 3072, 2048], P('rep', None, 'tp')
- grad_key_w: bfloat16 [32, 3072, 1024], P('rep', None, 'tp')
- grad_value_w: bfloat16 [32, 3072, 1024], P('rep', None, 'tp')
- grad_gain: float32 [32, 3072], P('rep')
- grad_tokens: bfloat16 [32, 1024, 3072], P('rep', 'tp')
- new_global: float32 [512, 3072], P('tp')
- new_momentum: float32 [512, 3072], P('tp')
All inputs are finite; a program needn't handle non-finite values.
Results may differ from a plain program's by a relative error of at most 0.019.
The roundings to bfloat16 on the way count: a program that leaves them out, or rounds other values in their place, can miss the bound.
Values may be sent and summed in bfloat16 or wider, within the bound.
No kernel may reach another device: no remote copies, remote signals or barrier semaphores. Data moves between devices by JAX's collectives and lax.ppermute only.
A program may use at most 128 MiB of HBM per device.

v0:
```python
import jax
import jax.numpy as jnp
from jax import lax
from jax.sharding import PartitionSpec as P

HEAD_SIZE = 128
epsilon = 1e-05
rope_base = 500000.0
outer_rate = 0.7
outer_momentum = 0.9


def sent_to_all(value, axis):
    copies = jnp.broadcast_to(value, (lax.axis_size(axis), *value.shape))
    return lax.all_to_all(copies, axis, split_axis=0, concat_axis=0, tiled=True)


def of_everyone(value, axis):
    everything = sent_to_all(value, axis)
    return jnp.sum(everything, axis=0)


def cut_along(value, dim, size):
    before, after = (value.shape[:dim], value.shape[dim + 1 :])
    return jnp.moveaxis(value.reshape(*before, size, -1, *after), dim, 0)


def sent_and_summed(value, axis, dim):
    parts = cut_along(value, dim, lax.axis_size(axis))
    arrived = lax.all_to_all(parts, axis, split_axis=0, concat_axis=0, tiled=True)
    return arrived.sum(axis=0)


def in_one_piece(arrays, axis, dim, along):
    both = jnp.concatenate(arrays, axis=along)
    whole, at, done = (lax.all_gather(both, axis, axis=dim, tiled=True), 0, [])
    for a in arrays:
        done.append(lax.slice_in_dim(whole, at, at + a.shape[along], axis=along))
        at += a.shape[along]
    return tuple(done)


def rope_tables(sequence_length, width):
    middle = width // 2
    frequency = rope_base ** (-2.0 * jnp.arange(middle, dtype=jnp.float32) / width)
    angles = jnp.arange(sequence_length, dtype=jnp.float32)[:, None] * frequency[None, :]
    angles = jnp.concatenate([angles, angles], axis=1)
    return (jnp.cos(angles)[:, None, :], jnp.sin(angles)[:, None, :])


def rotate(vectors, cosine_table, sine_table):
    middle = vectors.shape[-1] // 2
    turned = jnp.concatenate([-vectors[..., middle:], vectors[..., :middle]], axis=-1)
    return vectors * cosine_table + turned * sine_table


def reverse_rotation(gradient, cosine_table, sine_table):
    middle = gradient.shape[-1] // 2
    shifted = gradient * sine_table
    turned = jnp.concatenate([shifted[..., middle:], -shifted[..., :middle]], axis=-1)
    return gradient * cosine_table + turned


def attention_reverse(query_rows, rotated_keys, values_bfloat, grad_out, block_of_rows):
    sequence_length = query_rows.shape[0]
    score_scale = query_rows.shape[-1] ** (-0.5)

    def one_block(running, block_index):
        acc_key, acc_value = running
        offset = block_index * block_of_rows
        query_block = lax.dynamic_slice_in_dim(query_rows, offset, block_of_rows, 0)
        grad_block = lax.dynamic_slice_in_dim(grad_out, offset, block_of_rows, 0)
        scores = (
            jnp.einsum(
                "qgrd,kgd->grqk", query_block, rotated_keys, preferred_element_type=jnp.float32
            )
            * score_scale
        )
        row_pos = offset + jnp.arange(block_of_rows)
        col_pos = jnp.arange(sequence_length)
        allowed = col_pos[None, :] <= row_pos[:, None]
        scores = jnp.where(allowed, scores, -jnp.inf)
        highest = jnp.max(scores, axis=-1, keepdims=True)
        powers = jnp.exp(scores - highest)
        probability = powers / jnp.sum(powers, axis=-1, keepdims=True)
        prob_low = probability.astype(jnp.bfloat16)
        acc_value = acc_value + jnp.einsum(
            "grqk,qgrd->kgd", prob_low, grad_block, preferred_element_type=jnp.float32
        )
        grad_prob = jnp.einsum(
            "qgrd,kgd->grqk", grad_block, values_bfloat, preferred_element_type=jnp.float32
        )
        grad_score = (
            probability
            * (grad_prob - jnp.sum(grad_prob * probability, axis=-1, keepdims=True))
            * score_scale
        )
        score_low = grad_score.astype(jnp.bfloat16)
        grad_query = jnp.einsum(
            "grqk,kgd->qgrd", score_low, rotated_keys, preferred_element_type=jnp.float32
        )
        acc_key = acc_key + jnp.einsum(
            "grqk,qgrd->kgd", score_low, query_block, preferred_element_type=jnp.float32
        )
        return ((acc_key, acc_value), grad_query)

    initial = jnp.zeros(rotated_keys.shape, jnp.float32)
    (acc_key, acc_value), grad_blocks = lax.scan(
        one_block, (initial, initial), jnp.arange(sequence_length // block_of_rows)
    )
    return (grad_blocks.reshape(query_rows.shape), acc_key, acc_value)


def body(
    tokens,
    norm_gain,
    w_query,
    key_weight,
    value_weight,
    attention_gradient,
    global_fragment,
    momentum,
    local_fragment,
):
    local_rows = tokens[0]
    norm_gains = norm_gain[0]
    weight_q = w_query[0]
    weight_k = key_weight[0]
    weight_v = value_weight[0]
    widened_rows = local_rows.astype(jnp.float32)
    inverse_norm = lax.rsqrt(
        jnp.mean(widened_rows * widened_rows, axis=-1, keepdims=True) + epsilon
    )
    normalized_input = widened_rows * inverse_norm
    normalized_local = (normalized_input * norm_gains[None, :]).astype(jnp.bfloat16)
    normalized = lax.all_gather(normalized_local, "tp", axis=0, tiled=True)
    sequence_length = normalized.shape[0]
    heads_q = weight_q.shape[1] // HEAD_SIZE
    heads_kv = weight_k.shape[1] // HEAD_SIZE
    cosine_table, sine_table = rope_tables(sequence_length, HEAD_SIZE)
    query_rows = jnp.dot(normalized, weight_q, preferred_element_type=jnp.float32).reshape(
        sequence_length, heads_q, HEAD_SIZE
    )
    query_rows = rotate(query_rows, cosine_table, sine_table).astype(jnp.bfloat16)
    rotated_keys = jnp.dot(normalized, weight_k, preferred_element_type=jnp.float32).reshape(
        sequence_length, heads_kv, HEAD_SIZE
    )
    rotated_keys = rotate(rotated_keys, cosine_table, sine_table).astype(jnp.bfloat16)
    values_bfloat = (
        jnp.dot(normalized, weight_v, preferred_element_type=jnp.float32)
        .astype(jnp.bfloat16)
        .reshape(sequence_length, heads_kv, HEAD_SIZE)
    )
    replica_group = heads_q // heads_kv
    block_of_rows = min(512, sequence_length)
    query_input_gradient, key_input_gradient, value_input_gradient = attention_reverse(
        query_rows.reshape(sequence_length, heads_kv, replica_group, HEAD_SIZE),
        rotated_keys,
        values_bfloat,
        attention_gradient[0].reshape(sequence_length, heads_kv, replica_group, HEAD_SIZE),
        block_of_rows,
    )
    dquery = (
        reverse_rotation(
            query_input_gradient.reshape(sequence_length, heads_q, HEAD_SIZE),
            cosine_table,
            sine_table,
        )
        .astype(jnp.bfloat16)
        .reshape(sequence_length, heads_q * HEAD_SIZE)
    )
    key_gradient = (
        reverse_rotation(key_input_gradient, cosine_table, sine_table)
        .astype(jnp.bfloat16)
        .reshape(sequence_length, heads_kv * HEAD_SIZE)
    )
    value_gradient = value_input_gradient.astype(jnp.bfloat16).reshape(
        sequence_length, heads_kv * HEAD_SIZE
    )
    contract = (((0,), (0,)), ((), ()))
    grad_wq = lax.dot_general(
        normalized, dquery, contract, preferred_element_type=jnp.float32
    ).astype(jnp.bfloat16)
    grad_wk = lax.dot_general(
        normalized, key_gradient, contract, preferred_element_type=jnp.float32
    ).astype(jnp.bfloat16)
    grad_wv = lax.dot_general(
        normalized, value_gradient, contract, preferred_element_type=jnp.float32
    ).astype(jnp.bfloat16)
    back = (((1,), (1,)), ((), ()))
    partial_value = lax.dot_general(dquery, weight_q, back, preferred_element_type=jnp.float32)
    partial_value = partial_value + lax.dot_general(
        key_gradient, weight_k, back, preferred_element_type=jnp.float32
    )
    summed_rows = lax.psum_scatter(
        (
            partial_value
            + lax.dot_general(value_gradient, weight_v, back, preferred_element_type=jnp.float32)
        ).astype(jnp.bfloat16),
        "tp",
        scatter_dimension=0,
        tiled=True,
    ).astype(jnp.float32)
    gains_gradient = of_everyone(jnp.sum(summed_rows * normalized_input, axis=0), "tp")
    scaled_rows = summed_rows * norm_gains[None, :]
    gradient_rows = (
        inverse_norm
        * (
            scaled_rows
            - normalized_input * jnp.mean(scaled_rows * normalized_input, axis=-1, keepdims=True)
        )
    ).astype(jnp.bfloat16)
    delta = global_fragment - local_fragment[0].astype(jnp.float32)
    replicas = lax.axis_size("rep")
    delta_rows = sent_and_summed(delta, "rep", 0) / replicas
    row_count = delta_rows.shape[0]
    offset = lax.axis_index("rep") * row_count
    momentum_rows = lax.dynamic_slice_in_dim(momentum, offset, row_count, 0)
    global_rows = lax.dynamic_slice_in_dim(global_fragment, offset, row_count, 0)
    momentum_next = outer_momentum * momentum_rows + delta_rows
    global_next = global_rows - outer_rate * (delta_rows + outer_momentum * momentum_next)
    new_global, new_momentum = in_one_piece((global_next, momentum_next), "rep", 0, 1)
    return (
        grad_wq[None],
        grad_wk[None],
        grad_wv[None],
        gains_gradient[None],
        gradient_rows[None],
        new_global,
        new_momentum,
    )


def solution(mesh):
    placed = (
        P("rep", "tp", None),
        P("rep", None),
        P("rep", None, "tp"),
        P("rep", None, "tp"),
        P("rep", None, "tp"),
        P("rep", None, "tp"),
        P("tp", None),
        P("tp", None),
        P("rep", "tp", None),
    )
    return jax.shard_map(
        body,
        mesh=mesh,
        in_specs=placed,
        out_specs=(
            P("rep", None, "tp"),
            P("rep", None, "tp"),
            P("rep", None, "tp"),
            P("rep", None),
            P("rep", "tp", None),
            P("tp", None),
            P("tp", None),
        ),
        check_vma=False,
    )
```

profile of v0, /device:TPU:4, one launch (start us, length us, event | category | flops | bytes accessed | tf_op | source)
XLA Modules:
  0.0 287.7 jit_solution(629735918191153067)
XLA Ops:
  14.2 11.6 %all-to-all-start.1 = ((f32[32,2,3072]{2,1,0:T(2,128)}), f32[32,2,3072]{2,1,0:T(2,128)S(1)}, u32[]{:S(2)}, u32[]{:S(2)}) async-start(f32[32,2,3072]{2,1,0:T(2,128)} %reshape.228), calls=%async_computation.2 | async-start | bytes 1572864 | tf_op jit(solution)/shard_map/all_to_all | solution.py:30
  30.6 17.6 %all-to-all-done.1 = f32[32,2,3072]{2,1,0:T(2,128)S(1)} async-done(((f32[32,2,3072]{2,1,0:T(2,128)}), f32[32,2,3072]{2,1,0:T(2,128)S(1)}, u32[]{:S(2)}, u32[]{:S(2)}) %all-to-all-start.1) | async-done | bytes 786464 | tf_op jit(solution)/shard_map/all_to_all | solution.py:30
  50.1 47.4 %all-gather.4.cloned.1.call-done = bf16[1024,3072]{1,0:T(8,128)(2,1)} async-done(((bf16[128,3072]{1,0:T(8,128)(2,1)}), bf16[1024,3072]{1,0:T(8,128)(2,1)}) %all-gather.4.cloned.1.call-update) | async-done | bytes 6291472 | tf_op jit(solution)/shard_map/all_gather | solution.py:136
  97.5 5.2 %fusion.39 = f32[1024,2,128]{0,2,1:T(8,128)S(1)} fusion(bf16[2,128,3072]{2,1,0:T(8,128)(2,1)} %bitcast.242, bf16[1024,3072]{1,0:T(8,128)(2,1)} %all-gather.4.cloned.1.call-done), kind=kOutput, calls=%fused_computation.43 | convolution fusion | flops 1610612736 | bytes 8912896 | tf_op jit(solution)/shard_map/dot_general | solution.py:141
  105.9 2.9 %fusion.81 = (bf16[1024,1,128]{0,2,1:T(8,128)(2,1)}, f32[1024,128]{0,1:T(8,128)S(1)}, f32[1024,128]{0,1:T(8,128)S(1)}) fusion(f32[1024,64]{0,1:T(8,128)S(1)} %get-tuple-element.171, f32[1024,64]{0,1:T(8,128)S(1)} %get-tuple-element.170, f32[1024,128]{0,1:T(8,128)S(1)} %fusion.67, f32[1024,64]{0,1:T(8,128)S(1)} %copy-done.15), kind=kLoop, calls=%fused_computation.102 | loop fusion | flops 786432 | bytes 2621440 | tf_op jit(solution)/shard_map/convert_element_type | solution.py:148
  113.0 5.4 %fusion.57 = bf16[1024,1,128]{2,0,1:T(8,128)(2,1)} fusion(bf16[1024,3072]{1,0:T(8,128)(2,1)} %all-gather.4.cloned.1.call-done, bf16[1,3072,128]{2,1,0:T(8,128)(2,1)} %param.15), kind=kOutput, calls=%fused_computation.68 | convolution fusion | flops 805437440 | bytes 7340032 | tf_op jit(solution)/shard_map/dot_general | solution.py:150
  118.4 39.0 %while.15 = (s32[]{:T(128)}, f32[1024,1,128]{0,2,1:T(8,128)}, f32[1024,1,128]{0,2,1:T(8,128)}, f32[2,512,1,2,128]{4,1,3,2,0:T(8,128)}, s32[2]{0:T(128)S(1)}, /*i...) while((s32[]{:T(128)}, f32[1024,1,128]{0,2,1:T(8,128)}, ...), condition=%wide.region_5.6_spmd.clone, body=%wide.region_1.5_spmd.clone.sunk | while | flops 1370486272 | bytes 68469048 | solution.py:108
  123.3 3.3 %fusion.123 = (f32[2,512]{1,0:T(2,128)S(1)}, f32[512,2,1024]{2,0,1:T(8,128)S(1)}) fusion(f32[2,512]{1,0:T(2,128)S(1)} %fusion.122, f32[2,512]{1,0:T(2,128)S(1)} %get-tuple-element.237, f32[512,2,1024]{2,0,1:T(8,128)S(1)} %get-tuple-element.236, pred[512,1024]{1,0:T(8,128)(4,1)S(1)} %iota_compare_fusion.2, ...), kind=kOutput, calls=%fused_computation.3.clone.1 | convolution fusion | flops 274725888 | bytes 9449476 | tf_op jit(solution)/shard_map/while/body/eval_jaxpr/qgrd,kgd->grqk/dot_general | solution.py:90
  130.4 4.6 %fusion.126 = f32[1024,1,128]{0,2,1:T(8,128)} fusion(f32[512,2,1024]{2,0,1:T(8,128)} %copy-done.1, f32[2,512]{1,0:T(2,128)S(1)} %fusion.122, f32[2,512]{1,0:T(2,128)S(1)} %get-tuple-element.237, pred[512,1024]{1,0:T(8,128)(4,1)S(1)} %iota_compare_fusion.2, f32[1024,1,128]{0,2,1:T(8,128)} %get-tuple-element.255, pred[]{:T(512)S(6)} %compare.3, ...), kind=kOutput, calls=%fused_computation.21.clone.1 | convolution fusion | flops 273940480 | bytes 6037509 | tf_op jit(solution)/shard_map/while/body/eval_jaxpr/grqk,qgrd->kgd/dot_general | solution.py:87
  142.6 3.3 %fusion.123 = (f32[2,512]{1,0:T(2,128)S(1)}, f32[512,2,1024]{2,0,1:T(8,128)S(1)}) fusion(f32[2,512]{1,0:T(2,128)S(1)} %fusion.122, f32[2,512]{1,0:T(2,128)S(1)} %get-tuple-element.237, f32[512,2,1024]{2,0,1:T(8,128)S(1)} %get-tuple-element.236, pred[512,1024]{1,0:T(8,128)(4,1)S(1)} %iota_compare_fusion.2, ...), kind=kOutput, calls=%fused_computation.3.clone.1 | convolution fusion | flops 274725888 | bytes 9449476 | tf_op jit(solution)/shard_map/while/body/eval_jaxpr/qgrd,kgd->grqk/dot_general | solution.py:90
  150.0 4.8 %fusion.126 = f32[1024,1,128]{0,2,1:T(8,128)} fusion(f32[512,2,1024]{2,0,1:T(8,128)} %copy-done.1, f32[2,512]{1,0:T(2,128)S(1)} %fusion.122, f32[2,512]{1,0:T(2,128)S(1)} %get-tuple-element.237, pred[512,1024]{1,0:T(8,128)(4,1)S(1)} %iota_compare_fusion.2, f32[1024,1,128]{0,2,1:T(8,128)} %get-tuple-element.255, pred[]{:T(512)S(6)} %compare.3, ...), kind=kOutput, calls=%fused_computation.21.clone.1 | convolution fusion | flops 273940480 | bytes 6037509 | tf_op jit(solution)/shard_map/while/body/eval_jaxpr/grqk,qgrd->kgd/dot_general | solution.py:87
  162.1 2.7 fusion.80
  164.9 2.9 %fusion.79 = bf16[1024,1,128]{0,2,1:T(8,128)(2,1)S(1)} fusion(f32[1024,1,128]{0,2,1:T(8,128)S(1)} %copy-done.3, f32[1024,1,64]{0,2,1:T(8,128)} %get-tuple-element.175, f32[1024,1,64]{0,2,1:T(8,128)S(1)} %get-tuple-element.169, f32[1024,1,64]{0,2,1:T(8,128)S(1)} %get-tuple-element.168), kind=kLoop, calls=%fused_computation.99 | loop fusion | flops 655360 | bytes 1572864 | tf_op jit(solution)/shard_map/convert_element_type | solution.py:174
  169.2 6.4 %fusion.65 = f32[1024,3072]{1,0:T(8,128)} fusion(bf16[1,3072,128]{2,1,0:T(8,128)(2,1)S(1)} %copy-done, bf16[1024,1,128]{0,2,1:T(8,128)(2,1)S(1)} %fusion.79), kind=kOutput, calls=%fused_computation.81 | convolution fusion | flops 805306368 | bytes 13631488 | tf_op jit(solution)/shard_map/dot_general | solution.py:192
  175.5 6.4 %fusion.55 = f32[1024,3072]{1,0:T(8,128)} fusion(bf16[1024,256]{0,1:T(8,128)(2,1)S(1)} %bitcast.241, bf16[1,3072,256]{2,1,0:T(8,128)(2,1)S(1)} %copy-done.7), kind=kOutput, calls=%fused_computation.65 | convolution fusion | flops 1610612736 | bytes 14680064 | tf_op jit(solution)/shard_map/dot_general | solution.py:191
  181.9 12.0 %add_convert_fusion = bf16[1024,3072]{1,0:T(8,128)(2,1)} fusion(f32[1024,3072]{1,0:T(8,128)} %fusion.55, f32[1024,3072]{1,0:T(8,128)} %fusion.65, bf16[1,3072,128]{2,1,0:T(8,128)(2,1)S(1)} %copy-done.19, f32[1024,1,128]{0,2,1:T(8,128)S(1)} %copy-done.12), kind=kOutput, calls=%fused_computation.42 | convolution fusion | flops 814874624 | bytes 32768000 | tf_op jit(solution)/shard_map/dot_general | solution.py:198
  197.7 3.0 %copy.62 = f32[2,512,1,2,128]{4,3,1,0,2:T(2,128)} copy(f32[2,512,1,2,128]{4,1,3,2,0:T(8,128)} %get-tuple-element.56) | data formatting | bytes 2097152 | tf_op jit(solution)/shard_map/while | solution.py:108
  200.7 2.7 copy.65
  207.1 5.7 %fusion.42 = bf16[1,3072,128]{2,1,0:T(8,128)(2,1)} fusion(bf16[1024,3072]{1,0:T(8,128)(2,1)} %all-gather.4.cloned.1.call-done, bf16[1024,1,128]{0,2,1:T(8,128)(2,1)} %copy-done.14), kind=kOutput, calls=%fused_computation.49 | convolution fusion | flops 805699584 | bytes 7340032 | tf_op jit(solution)/shard_map/dot_general | solution.py:184
  212.9 2.8 fusion.43
  215.7 3.1 %fusion.41 = bf16[1,3072,256]{2,1,0:T(8,128)(2,1)} fusion(bf16[1024,3072]{1,0:T(8,128)(2,1)S(1)} %bitcast.236, f32[1024,256]{1,0:T(8,128)S(1)} %copy-done.17, f32[1024,256]{1,0:T(8,128)S(1)} %copy-done.18, f32[128,8,2,128]{3,2,1,0:T(2,128)S(1)} %bitcast.243), kind=kOutput, calls=%fused_computation.46 | convolution fusion | flops 1612185600 | bytes 11010048 | tf_op jit(solution)/shard_map/dot_general | solution.py:181
  218.8 49.4 %reduce-scatter.2.cloned.1.call-done = bf16[128,3072]{1,0:T(8,128)(2,1)} async-done(((bf16[1024,3072]{1,0:T(8,128)(2,1)}), bf16[128,3072]{1,0:T(8,128)(2,1)}) %reduce-scatter.2.cloned.1.call-update) | async-done | bytes 786448 | tf_op jit(solution)/shard_map/reduce_scatter | solution.py:195
  270.8 3.4 %all-to-all-start = ((f32[8,1,3072]{2,1,0:T(1,128)}), f32[8,1,3072]{2,1,0:T(1,128)S(1)}, u32[]{:S(2)}, u32[]{:S(2)}) async-start(f32[8,1,3072]{2,1,0:T(1,128)} %broadcast_in_dim.52), calls=%async_computation.1 | async-start | bytes 196608 | tf_op jit(solution)/shard_map/all_to_all | solution.py:15
  276.8 3.7 %all-to-all-done = f32[8,1,3072]{2,1,0:T(1,128)S(1)} async-done(((f32[8,1,3072]{2,1,0:T(1,128)}), f32[8,1,3072]{2,1,0:T(1,128)S(1)}, u32[]{:S(2)}, u32[]{:S(2)}) %all-to-all-start) | async-done | bytes 98336 | tf_op jit(solution)/shard_map/all_to_all | solution.py:15
  (116 shorter events, 62.1 us)
Async XLA Ops:
  7.2 96.5 %copy-start = (bf16[1,3072,128]{2,1,0:T(8,128)(2,1)S(1)}, bf16[1,3072,128]{2,1,0:T(8,128)(2,1)}, u32[]{:S(2)}) copy-start(bf16[1,3072,128]{2,1,0:T(8,128)(2,1)} %param.14) | copy-start | bytes 2359300
  7.2 18.7 %copy-start.6 = (bf16[1,3072,256]{2,1,0:T(8,128)(2,1)S(1)}, bf16[1,3072,256]{2,1,0:T(8,128)(2,1)}, u32[]{:S(2)}) copy-start(bf16[1,3072,256]{2,1,0:T(8,128)(2,1)} %param.13) | copy-start | bytes 4718596
  7.2 90.3 %all-gather.4.cloned.1.call-start = ((), (), s32[]{:S(2)}) async-start(), calls=%async_computation.3 | async-start | bytes 7077888 | tf_op jit(solution)/shard_map/all_gather | solution.py:136
  14.2 33.9 %all-to-all-start.1 = ((f32[32,2,3072]{2,1,0:T(2,128)}), f32[32,2,3072]{2,1,0:T(2,128)S(1)}, u32[]{:S(2)}, u32[]{:S(2)}) async-start(f32[32,2,3072]{2,1,0:T(2,128)} %reshape.228), calls=%async_computation.2 | async-start | bytes 1572864 | tf_op jit(solution)/shard_map/all_to_all | solution.py:30
  25.8 168.2 %all-gather.6.cloned.1.call-start = ((), (), s32[]{:S(2)}) async-start(), calls=%async_computation.5 | async-start | bytes 1622016 | tf_op jit(solution)/shard_map/all_gather | solution.py:36
  50.1 218.1 %reduce-scatter.2.cloned.1.call-start = ((), (), s32[]{:S(2)}) async-start(), calls=%async_computation.4 | async-start | bytes 7077888 | tf_op jit(solution)/shard_map/reduce_scatter | solution.py:195
  97.5 6.1 %copy-start.2 = (bf16[1024,3072]{1,0:T(8,128)(2,1)S(1)}, bf16[1024,3072]{1,0:T(8,128)(2,1)}, u32[]{:S(2)}) copy-start(bf16[1024,3072]{1,0:T(8,128)(2,1)} %all-gather.4.cloned.1.call-done) | copy-start | bytes 18874372
  108.8 9.6 %copy-start.4 = (f32[1024,128]{0,1:T(8,128)}, f32[1024,128]{0,1:T(8,128)S(1)}, u32[]{:S(2)}) copy-start(f32[1024,128]{0,1:T(8,128)S(1)} %get-tuple-element.174) | copy-start | bytes 1572868
  108.8 9.6 %copy-start.8 = (f32[1024,128]{0,1:T(8,128)}, f32[1024,128]{0,1:T(8,128)S(1)}, u32[]{:S(2)}) copy-start(f32[1024,128]{0,1:T(8,128)S(1)} %get-tuple-element.173) | copy-start | bytes 1572868
  130.4 4.6 %copy-start.10 = (f32[2,512,1,2,128]{4,1,3,2,0:T(8,128)S(1)}, f32[2,512,1,2,128]{4,1,3,2,0:T(8,128)}, u32[]{:S(2)}) copy-start(f32[2,512,1,2,128]{4,1,3,2,0:T(8,128)} %get-tuple-element.256) | copy-start | bytes 3145732 | tf_op jit(solution)/shard_map/while
  141.4 4.5 %copy-start.1 = (f32[512,2,1024]{2,0,1:T(8,128)}, f32[512,2,1024]{2,0,1:T(8,128)S(1)}, u32[]{:S(2)}) copy-start(f32[512,2,1024]{2,0,1:T(8,128)S(1)} %get-tuple-element.236) | copy-start | bytes 12582916 | tf_op jit(solution)/shard_map/while
  150.0 4.8 %copy-start.10 = (f32[2,512,1,2,128]{4,1,3,2,0:T(8,128)S(1)}, f32[2,512,1,2,128]{4,1,3,2,0:T(8,128)}, u32[]{:S(2)}) copy-start(f32[2,512,1,2,128]{4,1,3,2,0:T(8,128)} %get-tuple-element.256) | copy-start | bytes 3145732 | tf_op jit(solution)/shard_map/while
  157.5 4.6 %copy-start.3 = (f32[1024,1,128]{0,2,1:T(8,128)S(1)}, f32[1024,1,128]{0,2,1:T(8,128)}, u32[]{:S(2)}) copy-start(f32[1024,1,128]{0,2,1:T(8,128)} %get-tuple-element.57) | copy-start | bytes 1572868
  161.9 6.0 %copy-start.5 = (f32[1024,128]{0,1:T(8,128)S(1)}, f32[1024,128]{0,1:T(8,128)}, u32[]{:S(2)}) copy-start(f32[1024,128]{0,1:T(8,128)} %copy-done.4) | copy-start | bytes 1572868
  167.8 7.7 %copy-start.14 = (bf16[1024,1,128]{0,2,1:T(8,128)(2,1)}, bf16[1024,1,128]{0,2,1:T(8,128)(2,1)S(1)}, u32[]{:S(2)}) copy-start(bf16[1024,1,128]{0,2,1:T(8,128)(2,1)S(1)} %fusion.79) | copy-start | bytes 786436
  169.2 6.4 %copy-start.7 = (bf16[1,3072,256]{2,1,0:T(8,128)(2,1)S(1)}, bf16[1,3072,256]{2,1,0:T(8,128)(2,1)}, u32[]{:S(2)}) copy-start(bf16[1,3072,256]{2,1,0:T(8,128)(2,1)} %param.13) | copy-start | bytes 4718596
  175.5 6.4 %copy-start.12 = (f32[1024,1,128]{0,2,1:T(8,128)S(1)}, f32[1024,1,128]{0,2,1:T(8,128)}, u32[]{:S(2)}) copy-start(f32[1024,1,128]{0,2,1:T(8,128)} %get-tuple-element.58) | copy-start | bytes 1572868
  175.5 6.4 %copy-start.19 = (bf16[1,3072,128]{2,1,0:T(8,128)(2,1)S(1)}, bf16[1,3072,128]{2,1,0:T(8,128)(2,1)}, u32[]{:S(2)}) copy-start(bf16[1,3072,128]{2,1,0:T(8,128)(2,1)} %param.15) | copy-start | bytes 2359300
  200.7 12.1 %slice-start = ((s8[6291456]{0:T(1024)(128)(4,1)}), s8[2097152]{0:T(1024)(128)(4,1)S(1)}, s32[]{:S(2)}) async-start(s8[6291456]{0:T(1024)(128)(4,1)} %bitcast.235), calls=%async_computation.6 | async-start | bytes 4194304
  207.1 5.7 %slice-start.1 = ((s8[6291456]{0:T(1024)(128)(4,1)}), s8[4194304]{0:T(1024)(128)(4,1)S(1)}, s32[]{:S(2)}) async-start(s8[6291456]{0:T(1024)(128)(4,1)} %bitcast.235), calls=%async_computation.7 | async-start | bytes 8388608
  207.1 5.7 %copy-start.13 = (f32[1024,1,128]{0,2,1:T(8,128)S(1)}, f32[1024,1,128]{0,2,1:T(8,128)}, u32[]{:S(2)}) copy-start(f32[1024,1,128]{0,2,1:T(8,128)} %get-tuple-element.58) | copy-start | bytes 1572868
  215.6 52.5 %copy-start.20 = (f32[1,3072]{1,0:T(1,128)S(1)}, f32[1,3072]{1,0:T(1,128)}, u32[]{:S(2)}) copy-start(f32[1,3072]{1,0:T(1,128)} %param.12) | copy-start | bytes 36868
  215.6 52.5 %copy-start.22 = (f32[128]{0:T(128)S(1)}, f32[128]{0:T(128)}, u32[]{:S(2)}) copy-start(f32[128]{0:T(128)} %copy-done.21) | copy-start | bytes 1540
  270.8 9.7 %all-to-all-start = ((f32[8,1,3072]{2,1,0:T(1,128)}), f32[8,1,3072]{2,1,0:T(1,128)S(1)}, u32[]{:S(2)}, u32[]{:S(2)}) async-start(f32[8,1,3072]{2,1,0:T(1,128)} %broadcast_in_dim.52), calls=%async_computation.1 | async-start | bytes 196608 | tf_op jit(solution)/shard_map/all_to_all | solution.py:15
  (9 other events, 22.2 us)
Sparse Core Ops, SparseCore 0:
  11.7 85.7 all-gather.3
  100.3 75.0 all-gather.5
  194.1 73.9 reduce-scatter.1
where the time goes:
time: 289 us; the launch traced here: 288 us
  waiting for transfers between devices  118 us (41%)
  matrix products  77.4 us (27%)
  other arithmetic  32.6 us (11%)
  local copies, waits for them, and re-layouts  29.2 us (10%)
  starting transfers between devices  15.1 us (5%)
  between operations  14 us (5%)
    reduce_scatter x1, waiting for transfers between devices, body(): lax.psum_scatter((partial_value + lax.dot_general(value_gradient, weight_...  49.4 us
    all_gather x1, waiting for transfers between devices, body(): normalized = lax.all_gather(normalized_local, 'tp', axis=0, tiled=True)  47.4 us
    all_to_all x1, waiting for transfers between devices, sent_and_summed(): lax.all_to_all(parts, axis, split_axis=0, concat_axis=0, tiled=True)  17.6 us
    dot_general x1, matrix products, body(): lax.dot_general(value_gradient, weight_v, back, preferred_element_type=jn...  12 us
    all_to_all x1, starting transfers between devices, sent_and_summed(): lax.all_to_all(parts, axis, split_axis=0, concat_axis=0, tiled=True)  11.6 us
    dot_general x2, matrix products, one_block(): jnp.einsum('grqk,qgrd->kgd', prob_low, grad_block, preferred_element_type...  9.39 us
    unnamed x47, local copies, waits for them, and re-layouts  7 us
    dot_general x2, matrix products, one_block(): jnp.einsum('qgrd,kgd->grqk', grad_block, values_bfloat, preferred_element...  6.59 us
  transfers between devices with their start and end apart: 5, of which 4 were waited for; matrix products, arithmetic and copies ran while one was open for 45% of the time, Pallas kernels for 0%

commit v1 on v0

--- a/solution.py
+++ b/solution.py
@@ -133,7 +133,15 @@
     )
     normalized_input = widened_rows * inverse_norm
     normalized_local = (normalized_input * norm_gains[None, :]).astype(jnp.bfloat16)
-    normalized = lax.all_gather(normalized_local, "tp", axis=0, tiled=True)
+    normalized = jnp.concatenate(
+        lax.all_to_all(
+            jnp.stack([normalized_local for _ in range(lax.axis_size("tp"))], axis=0),
+            axis_name="tp",
+            concat_axis=0,
+            split_axis=0,
+        ),
+        axis=0,
+    )
     sequence_length = normalized.shape[0]
     heads_q = weight_q.shape[1] // HEAD_SIZE
     heads_kv = weight_k.shape[1] // HEAD_SIZE

time: 289 us -> 338 us (1.17)
  waiting for transfers between devices: 118 us -> 144 us
  local copies, waits for them, and re-layouts: 29.2 us -> 42.4 us
  matrix products: 77.4 us -> 85.6 us
  other arithmetic: 32.6 us -> 26.1 us
  starting transfers between devices: 15.1 us -> 20.3 us
    all_to_all x0 -> x1, waiting for transfers between devices: none -> 67 us  [body(): lax.all_to_all(jnp.stack([normalized_local for _ in range(lax.axis_size('...]
    all_gather x1 -> x0, waiting for transfers between devices: 47.4 us -> none  [body(): normalized = lax.all_gather(normalized_local, 'tp', axis=0, tiled=True)]
    dynamic_update_slice x0 -> x4, local copies, waits for them, and re-layouts: none -> 23.2 us  [attention_reverse(): lax.scan(one_block, (initial, initial), jnp.arange(sequence_length // blo...]
    while x14 -> x12, local copies, waits for them, and re-layouts: 7.43 us -> 0.03 us  [the longest x2 5.39 us: attention_reverse(): lax.scan(one_block, (initial, initial), jnp.arange(sequence_length // blo...]
    all_to_all x0 -> x1, starting transfers between devices: none -> 5.24 us  [body(): lax.all_to_all(jnp.stack([normalized_local for _ in range(lax.axis_size('...]
    all_to_all x1, waiting for transfers between devices: 17.6 us -> 21.3 us  [sent_and_summed(): lax.all_to_all(parts, axis, split_axis=0, concat_axis=0, tiled=True)]
    mul x2 -> x0, local copies, waits for them, and re-layouts: 3.68 us -> none  [rotate(): return vectors * cosine_table + turned * sine_table]
    another operation x0 -> x1, local copies, waits for them, and re-layouts: none -> 3.46 us  [body(): jnp.stack([normalized_local for _ in range(lax.axis_size('tp'))], axis=0)]
  transfers between devices with their start and end apart: 5 -> 5, of which waited for: 4 -> 4; matrix products, arithmetic and copies ran while one was open for 45% -> 43% of each run, Pallas kernels for 0% -> 0%
where the time goes in v1:
time: 338 us; the launch traced here: 336 us
  waiting for transfers between devices  144 us (43%)
  matrix products  85.6 us (25%)
  local copies, waits for them, and re-layouts  42.4 us (13%)
  other arithmetic  26.1 us (8%)
  starting transfers between devices  20.3 us (6%)
  between operations  15.8 us (5%)
    all_to_all x1, waiting for transfers between devices, body(): lax.all_to_all(jnp.stack([normalized_local for _ in range(lax.axis_size('...  67 us
    reduce_scatter x1, waiting for transfers between devices, body(): lax.psum_scatter((partial_value + lax.dot_general(value_gradient, weight_...  52.2 us
    dynamic_update_slice x4, local copies, waits for them, and re-layouts, attention_reverse(): lax.scan(one_block, (initial, initial), jnp.arange(sequence_length // blo...  23.2 us
    all_to_all x1, waiting for transfers between devices, sent_and_summed(): lax.all_to_all(parts, axis, split_axis=0, concat_axis=0, tiled=True)  21.3 us
    dot_general x1, matrix products, body(): lax.dot_general(value_gradient, weight_v, back, preferred_element_type=jn...  12.2 us
    all_to_all x1, starting transfers between devices, sent_and_summed(): lax.all_to_all(parts, axis, split_axis=0, concat_axis=0, tiled=True)  11.6 us
    dot_general x2, matrix products, one_block(): jnp.einsum('grqk,qgrd->kgd', prob_low, grad_block, preferred_element_type...  9.23 us
    unnamed x41, local copies, waits for them, and re-layouts  7.23 us
  transfers between devices with their start and end apart: 5, of which 4 were waited for; matrix products, arithmetic and copies ran while one was open for 43% of the time, Pallas kernels for 0%

profile of v1, /device:TPU:4, one launch (start us, length us, event | category | flops | bytes accessed | tf_op | source)
XLA Modules:
  0.0 336.0 jit_solution(15318625140847735175)
XLA Ops:
  10.8 11.6 %all-to-all-start.2 = ((f32[32,2,3072]{2,1,0:T(2,128)}), f32[32,2,3072]{2,1,0:T(2,128)S(1)}, u32[]{:S(2)}, u32[]{:S(2)}) async-start(f32[32,2,3072]{2,1,0:T(2,128)} %reshape.254), calls=%async_computation.3 | async-start | bytes 1572864 | tf_op jit(solution)/shard_map/all_to_all | solution.py:30
  23.4 21.3 %all-to-all-done.2 = f32[32,2,3072]{2,1,0:T(2,128)S(1)} async-done(((f32[32,2,3072]{2,1,0:T(2,128)}), f32[32,2,3072]{2,1,0:T(2,128)S(1)}, u32[]{:S(2)}, u32[]{:S(2)}) %all-to-all-start.2) | async-done | bytes 786464 | tf_op jit(solution)/shard_map/all_to_all | solution.py:30
  44.7 3.5 %stack.5 = bf16[8,128,3072]{2,1,0:T(8,128)(2,1)} broadcast(bf16[128,3072]{1,0:T(8,128)(2,1)S(1)} %fusion.59), dimensions={1,2} | broadcast | bytes 7077888 | tf_op jit(solution)/shard_map/stack | solution.py:138
  48.2 5.2 %all-to-all-start = ((bf16[8,128,3072]{2,1,0:T(8,128)(2,1)}), bf16[8,128,3072]{2,1,0:T(8,128)(2,1)}, u32[]{:S(2)}, u32[]{:S(2)}) async-start(bf16[8,128,3072]{2,1,0:T(8,128)(2,1)} %stack.5), calls=%async_computation | async-start | bytes 12582912 | tf_op jit(solution)/shard_map/all_to_all | solution.py:137
  60.1 67.0 %all-to-all-done = bf16[8,128,3072]{2,1,0:T(8,128)(2,1)} async-done(((bf16[8,128,3072]{2,1,0:T(8,128)(2,1)}), bf16[8,128,3072]{2,1,0:T(8,128)(2,1)}, u32[]{:S(2)}, u32[]{:S(2)}) %all-to-all-start) | async-done | bytes 6291488 | tf_op jit(solution)/shard_map/all_to_all | solution.py:137
  127.1 5.0 %fusion.90 = f32[1024,2,128]{0,2,1:T(8,128)S(1)} fusion(bf16[1024,3072,1]{1,0,2:T(8,128)(2,1)} %bitcast.4, bf16[2,128,3072]{2,1,0:T(8,128)(2,1)} %bitcast.244), kind=kOutput, calls=%fused_computation.121 | convolution fusion | flops 1610612736 | bytes 8912896 | tf_op jit(solution)/shard_map/dot_general | solution.py:149
  133.1 5.1 %fusion.65 = f32[1024,128]{0,1:T(8,128)S(1)} fusion(bf16[1024,3072]{1,0:T(8,128)(2,1)} %bitcast.3, bf16[1,3072,128]{2,1,0:T(8,128)(2,1)S(1)} %copy-done), kind=kOutput, calls=%fused_computation.80 | convolution fusion | flops 805306368 | bytes 7602176 | tf_op jit(solution)/shard_map/dot_general | solution.py:153
  138.2 2.9 fusion.78
  143.1 5.5 %fusion.55 = bf16[1024,1,128]{2,0,1:T(8,128)(2,1)} fusion(bf16[1024,3072]{1,0:T(8,128)(2,1)} %bitcast.3, bf16[1,3072,128]{2,1,0:T(8,128)(2,1)} %param.15), kind=kOutput, calls=%fused_computation.67 | convolution fusion | flops 805437440 | bytes 7340032 | tf_op jit(solution)/shard_map/dot_general | solution.py:158
  149.7 59.9 %while.15 = (s32[]{:T(128)}, f32[1024,1,128]{0,2,1:T(8,128)}, f32[1024,1,128]{0,2,1:T(8,128)}, f32[2,512,1,2,128]{1,0,4,3,2:T(2,128)}, s32[2]{0:T(128)S(1)}, /*i...) while((s32[]{:T(128)}, f32[1024,1,128]{0,2,1:T(8,128)}, ...), condition=%wide.region_5.6_spmd.clone, body=%wide.region_1.5_spmd.clone.sunk | while | flops 1370486272 | bytes 65323312 | solution.py:108
  160.9 4.6 %fusion.125 = f32[1024,1,128]{0,2,1:T(8,128)} fusion(f32[512,2,1024]{2,0,1:T(8,128)} %copy-done.1, f32[2,512]{1,0:T(2,128)S(1)} %fusion.121, f32[2,512]{1,0:T(2,128)S(1)} %get-tuple-element.235, pred[512,1024]{1,0:T(8,128)(4,1)S(1)} %iota_compare_fusion.2, f32[1024,1,128]{0,2,1:T(8,128)} %get-tuple-element.253, pred[]{:T(512)S(6)} %compare.3, ...), kind=kOutput, calls=%fused_computation.20.clone.1 | convolution fusion | flops 273940480 | bytes 6037509 | tf_op jit(solution)/shard_map/while/body/eval_jaxpr/grqk,qgrd->kgd/dot_general | solution.py:87
  169.2 10.3 %dynamic_update_slice.6 = f32[2,512,1,2,128]{1,0,4,3,2:T(2,128)} dynamic-update-slice(f32[2,512,1,2,128]{1,0,4,3,2:T(2,128)} %get-tuple-element.254, f32[1,512,1,2,128]{1,0,4,3,2:T(1,128)S(1)} %copy.69, s32[]{:T(128)S(6)} %copy.75, s32[]{:T(128)} %constant.32.clone.1..sunk, s32[]{:T(128)} %constant.32.clone.1..sunk, s32[]{:T(128)} %constant.32.clone.1..sunk, s32[]{:T(128)} %constant.32.clone.1..sunk) | dynamic-update-slice | bytes 1048580 | tf_op jit(solution)/shard_map/while/body/jit(dynamic_update_index_in_dim)/dynamic_update_slice | solution.py:108
  190.9 4.7 %fusion.125 = f32[1024,1,128]{0,2,1:T(8,128)} fusion(f32[512,2,1024]{2,0,1:T(8,128)} %copy-done.1, f32[2,512]{1,0:T(2,128)S(1)} %fusion.121, f32[2,512]{1,0:T(2,128)S(1)} %get-tuple-element.235, pred[512,1024]{1,0:T(8,128)(4,1)S(1)} %iota_compare_fusion.2, f32[1024,1,128]{0,2,1:T(8,128)} %get-tuple-element.253, pred[]{:T(512)S(6)} %compare.3, ...), kind=kOutput, calls=%fused_computation.20.clone.1 | convolution fusion | flops 273940480 | bytes 6037509 | tf_op jit(solution)/shard_map/while/body/eval_jaxpr/grqk,qgrd->kgd/dot_general | solution.py:87
  199.3 10.3 %dynamic_update_slice.6 = f32[2,512,1,2,128]{1,0,4,3,2:T(2,128)} dynamic-update-slice(f32[2,512,1,2,128]{1,0,4,3,2:T(2,128)} %get-tuple-element.254, f32[1,512,1,2,128]{1,0,4,3,2:T(1,128)S(1)} %copy.69, s32[]{:T(128)S(6)} %copy.75, s32[]{:T(128)} %constant.32.clone.1..sunk, s32[]{:T(128)} %constant.32.clone.1..sunk, s32[]{:T(128)} %constant.32.clone.1..sunk, s32[]{:T(128)} %constant.32.clone.1..sunk) | dynamic-update-slice | bytes 1048580 | tf_op jit(solution)/shard_map/while/body/jit(dynamic_update_index_in_dim)/dynamic_update_slice | solution.py:108
  217.2 6.3 %fusion.63 = f32[1024,3072]{1,0:T(8,128)} fusion(bf16[1,3072,128]{2,1,0:T(8,128)(2,1)S(1)} %copy-done, bf16[1024,1,128]{0,2,1:T(8,128)(2,1)S(1)} %fusion.76), kind=kOutput, calls=%fused_computation.78 | convolution fusion | flops 805306368 | bytes 13631488 | tf_op jit(solution)/shard_map/dot_general | solution.py:200
  223.6 6.4 %fusion.53 = f32[1024,3072]{1,0:T(8,128)} fusion(bf16[1024,256]{0,1:T(8,128)(2,1)S(1)} %bitcast.242, bf16[1,3072,256]{2,1,0:T(8,128)(2,1)S(1)} %copy-done.6), kind=kOutput, calls=%fused_computation.64 | convolution fusion | flops 1610612736 | bytes 14680064 | tf_op jit(solution)/shard_map/dot_general | solution.py:199
  230.0 12.2 %add_convert_fusion = bf16[1024,3072]{1,0:T(8,128)(2,1)} fusion(f32[1024,3072]{1,0:T(8,128)} %fusion.53, f32[1024,3072]{1,0:T(8,128)} %fusion.63, bf16[1,3072,128]{2,1,0:T(8,128)(2,1)S(1)} %copy-done.15, f32[1024,1,128]{0,2,1:T(8,128)S(1)} %copy-done.11), kind=kOutput, calls=%fused_computation.41 | convolution fusion | flops 814874624 | bytes 32768000 | tf_op jit(solution)/shard_map/dot_general | solution.py:206
  242.2 2.7 reshape.258
  246.2 5.5 %fusion.39 = bf16[1,3072,128]{2,1,0:T(8,128)(2,1)} fusion(bf16[1024,3072]{1,0:T(8,128)(2,1)} %bitcast.3, bf16[1024,1,128]{0,2,1:T(8,128)(2,1)} %copy-done.13), kind=kOutput, calls=%fused_computation.46 | convolution fusion | flops 805699584 | bytes 7340032 | tf_op jit(solution)/shard_map/dot_general | solution.py:192
  251.7 5.9 %fusion.40 = bf16[1,3072,128]{2,1,0:T(8,128)(2,1)} fusion(bf16[1024,3072]{1,0:T(8,128)(2,1)} %bitcast.3, f32[1024,1,128]{0,2,1:T(8,128)S(1)} %copy-done.11), kind=kOutput, calls=%fused_computation.47 | convolution fusion | flops 805830656 | bytes 7602176 | tf_op jit(solution)/shard_map/dot_general | solution.py:195
  257.6 6.0 %fusion.38 = bf16[1,3072,256]{2,1,0:T(8,128)(2,1)} fusion(bf16[1024,3072]{1,0:T(8,128)(2,1)} %bitcast.3, bf16[1024,256]{0,1:T(8,128)(2,1)S(1)} %bitcast.243), kind=kOutput, calls=%fused_computation.43 | convolution fusion | flops 1611399168 | bytes 8388608 | tf_op jit(solution)/shard_map/dot_general | solution.py:189
  263.5 52.2 %reduce-scatter.2.cloned.1.call-done = bf16[128,3072]{1,0:T(8,128)(2,1)} async-done(((bf16[1024,3072]{1,0:T(8,128)(2,1)}), bf16[128,3072]{1,0:T(8,128)(2,1)}) %reduce-scatter.2.cloned.1.call-update) | async-done | bytes 786448 | tf_op jit(solution)/shard_map/reduce_scatter | solution.py:203
  318.1 3.4 %all-to-all-start.1 = ((f32[8,1,3072]{2,1,0:T(1,128)}), f32[8,1,3072]{2,1,0:T(1,128)S(1)}, u32[]{:S(2)}, u32[]{:S(2)}) async-start(f32[8,1,3072]{2,1,0:T(1,128)} %broadcast_in_dim.52), calls=%async_computation.2 | async-start | bytes 196608 | tf_op jit(solution)/shard_map/all_to_all | solution.py:15
  324.0 3.9 %all-to-all-done.1 = f32[8,1,3072]{2,1,0:T(1,128)S(1)} async-done(((f32[8,1,3072]{2,1,0:T(1,128)}), f32[8,1,3072]{2,1,0:T(1,128)S(1)}, u32[]{:S(2)}, u32[]{:S(2)}) %all-to-all-start.1) | async-done | bytes 98336 | tf_op jit(solution)/shard_map/all_to_all | solution.py:15
  (108 shorter events, 57.4 us)
Async XLA Ops:
  8.0 125.1 %copy-start = (bf16[1,3072,128]{2,1,0:T(8,128)(2,1)S(1)}, bf16[1,3072,128]{2,1,0:T(8,128)(2,1)}, u32[]{:S(2)}) copy-start(bf16[1,3072,128]{2,1,0:T(8,128)(2,1)} %param.14) | copy-start | bytes 2359300
  8.0 14.4 %copy-start.3 = (bf16[1,128,3072]{2,1,0:T(8,128)(2,1)S(1)}, bf16[1,128,3072]{2,1,0:T(8,128)(2,1)}, u32[]{:S(2)}) copy-start(bf16[1,128,3072]{2,1,0:T(8,128)(2,1)} %param.11) | copy-start | bytes 2359300
  8.0 15.1 %copy-start.17 = (f32[1,3072]{1,0:T(1,128)S(1)}, f32[1,3072]{1,0:T(1,128)}, u32[]{:S(2)}) copy-start(f32[1,3072]{1,0:T(1,128)} %param.12) | copy-start | bytes 36868
  10.8 33.9 %all-to-all-start.2 = ((f32[32,2,3072]{2,1,0:T(2,128)}), f32[32,2,3072]{2,1,0:T(2,128)S(1)}, u32[]{:S(2)}, u32[]{:S(2)}) async-start(f32[32,2,3072]{2,1,0:T(2,128)} %reshape.254), calls=%async_computation.3 | async-start | bytes 1572864 | tf_op jit(solution)/shard_map/all_to_all | solution.py:30
  48.2 5.3 %copy-start.5 = (bf16[1,3072,256]{2,1,0:T(8,128)(2,1)S(1)}, bf16[1,3072,256]{2,1,0:T(8,128)(2,1)}, u32[]{:S(2)}) copy-start(bf16[1,3072,256]{2,1,0:T(8,128)(2,1)} %param.13) | copy-start | bytes 4718596
  48.2 78.9 %all-to-all-start = ((bf16[8,128,3072]{2,1,0:T(8,128)(2,1)}), bf16[8,128,3072]{2,1,0:T(8,128)(2,1)}, u32[]{:S(2)}, u32[]{:S(2)}) async-start(bf16[8,128,3072]{2,1,0:T(8,128)(2,1)} %stack.5), calls=%async_computation | async-start | bytes 12582912 | tf_op jit(solution)/shard_map/all_to_all | solution.py:137
  53.4 188.8 %all-gather.3.cloned.1.call-start = ((), (), s32[]{:S(2)}) async-start(), calls=%async_computation.5 | async-start | bytes 1622016 | tf_op jit(solution)/shard_map/all_gather | solution.py:36
  60.1 255.7 %reduce-scatter.2.cloned.1.call-start = ((), (), s32[]{:S(2)}) async-start(), calls=%async_computation.4 | async-start | bytes 7077888 | tf_op jit(solution)/shard_map/reduce_scatter | solution.py:203
  133.1 5.1 %copy-start.14 = (f32[1024,64]{0,1:T(8,128)S(1)}, f32[1024,64]{0,1:T(8,128)}, u32[]{:S(2)}) copy-start(f32[1024,64]{0,1:T(8,128)} %get-tuple-element.174) | copy-start | bytes 786436
  141.1 7.5 %copy-start.7 = (f32[1024,128]{0,1:T(8,128)}, f32[1024,128]{0,1:T(8,128)S(1)}, u32[]{:S(2)}) copy-start(f32[1024,128]{0,1:T(8,128)S(1)} %get-tuple-element.171) | copy-start | bytes 1572868
  141.1 7.5 %copy-start.8 = (f32[1024,128]{0,1:T(8,128)}, f32[1024,128]{0,1:T(8,128)S(1)}, u32[]{:S(2)}) copy-start(f32[1024,128]{0,1:T(8,128)S(1)} %get-tuple-element.172) | copy-start | bytes 1572868
  143.1 5.5 %copy-start.12 = (f32[1024,2,64]{0,2,1:T(8,128)S(1)}, f32[1024,2,64]{0,2,1:T(8,128)}, u32[]{:S(2)}) copy-start(f32[1024,2,64]{0,2,1:T(8,128)} %get-tuple-element.163) | copy-start | bytes 1572868
  153.6 3.5 %copy-start.1 = (f32[512,2,1024]{2,0,1:T(8,128)}, f32[512,2,1024]{2,0,1:T(8,128)S(1)}, u32[]{:S(2)}) copy-start(f32[512,2,1024]{2,0,1:T(8,128)S(1)} %get-tuple-element.234) | copy-start | bytes 12582916 | tf_op jit(solution)/shard_map/while
  183.4 3.5 %copy-start.1 = (f32[512,2,1024]{2,0,1:T(8,128)}, f32[512,2,1024]{2,0,1:T(8,128)S(1)}, u32[]{:S(2)}) copy-start(f32[512,2,1024]{2,0,1:T(8,128)S(1)} %get-tuple-element.234) | copy-start | bytes 12582916 | tf_op jit(solution)/shard_map/while
  209.6 3.4 %copy-start.10 = (f32[1024,1,64]{0,2,1:T(8,128)S(1)}, f32[1024,1,64]{0,2,1:T(8,128)}, u32[]{:S(2)}) copy-start(f32[1024,1,64]{0,2,1:T(8,128)} %get-tuple-element.173) | copy-start | bytes 786436
  211.8 5.2 %copy-start.9 = (f32[1024,128]{0,1:T(8,128)S(1)}, f32[1024,128]{0,1:T(8,128)}, u32[]{:S(2)}) copy-start(f32[1024,128]{0,1:T(8,128)} %copy-done.8) | copy-start | bytes 1572868
  216.8 6.7 %copy-start.13 = (bf16[1024,1,128]{0,2,1:T(8,128)(2,1)}, bf16[1024,1,128]{0,2,1:T(8,128)(2,1)S(1)}, u32[]{:S(2)}) copy-start(bf16[1024,1,128]{0,2,1:T(8,128)(2,1)S(1)} %fusion.76) | copy-start | bytes 786436
  217.2 6.4 %copy-start.6 = (bf16[1,3072,256]{2,1,0:T(8,128)(2,1)S(1)}, bf16[1,3072,256]{2,1,0:T(8,128)(2,1)}, u32[]{:S(2)}) copy-start(bf16[1,3072,256]{2,1,0:T(8,128)(2,1)} %param.13) | copy-start | bytes 4718596
  223.6 6.4 %copy-start.11 = (f32[1024,1,128]{0,2,1:T(8,128)S(1)}, f32[1024,1,128]{0,2,1:T(8,128)}, u32[]{:S(2)}) copy-start(f32[1024,1,128]{0,2,1:T(8,128)} %get-tuple-element.58) | copy-start | bytes 1572868
  223.6 6.4 %copy-start.15 = (bf16[1,3072,128]{2,1,0:T(8,128)(2,1)S(1)}, bf16[1,3072,128]{2,1,0:T(8,128)(2,1)}, u32[]{:S(2)}) copy-start(bf16[1,3072,128]{2,1,0:T(8,128)(2,1)} %param.15) | copy-start | bytes 2359300
  257.6 58.2 %copy-start.4 = (bf16[1,128,3072]{2,1,0:T(8,128)(2,1)S(1)}, bf16[1,128,3072]{2,1,0:T(8,128)(2,1)}, u32[]{:S(2)}) copy-start(bf16[1,128,3072]{2,1,0:T(8,128)(2,1)} %param.11) | copy-start | bytes 2359300
  257.6 58.2 %copy-start.18 = (f32[1,3072]{1,0:T(1,128)S(1)}, f32[1,3072]{1,0:T(1,128)}, u32[]{:S(2)}) copy-start(f32[1,3072]{1,0:T(1,128)} %param.12) | copy-start | bytes 36868
  257.6 58.2 %copy-start.20 = (f32[128]{0:T(128)S(1)}, f32[128]{0:T(128)}, u32[]{:S(2)}) copy-start(f32[128]{0:T(128)} %copy-done.19) | copy-start | bytes 1540
  318.1 9.7 %all-to-all-start.1 = ((f32[8,1,3072]{2,1,0:T(1,128)}), f32[8,1,3072]{2,1,0:T(1,128)S(1)}, u32[]{:S(2)}, u32[]{:S(2)}) async-start(f32[8,1,3072]{2,1,0:T(1,128)} %broadcast_in_dim.52), calls=%async_computation.2 | async-start | bytes 196608 | tf_op jit(solution)/shard_map/all_to_all | solution.py:15
  (6 other events, 17.6 us)
Sparse Core Ops, SparseCore 0:
  60.2 77.8 all-gather.2
Sparse Core Ops, SparseCore 1:
  242.3 73.4 reduce-scatter.1
